TPU v7x, 32 devices: a whole 2x2x4 slice. The times are simulated.
32 devices in a mesh: gx: 4 (over y, core), gy: 8 (over z, x).
Axes of the slice: x: 2, y: 2, z: 4, core: 2. Of those that a mesh axis runs over, the one named last changes fastest.
Arguments:
- right_side: float32 [128, 256, 512], P('gx', 'gy'), as said below
- start_guess: float32 [128, 256, 512], P('gx', 'gy'), may hold values from -3 to 3
- conductivity: float32 [128, 256, 512], P('gx', 'gy'), may hold values from 0.5 to 8
Outputs:
- solution_field: float32 [128, 256, 512], P('gx', 'gy')
- estimate: float32 [], replicated
Inputs may be any that keep to these rules, and one draw needn't show every extreme that they name: `right_side`: A smoothly varying positive scale times noise, which may have a nonzero mean.
All inputs are finite; a program needn't handle non-finite values.
Results may differ from a plain program's by a relative error of at most 0.0003.
Values sent between devices are 32-bit elements; how exact they have to be, the bound alone decides.
No kernel may reach another device: no remote copies, remote signals or barrier semaphores. Data moves between devices by JAX's collectives and lax.ppermute only.
A program may use at most 64 MiB of HBM per device.

v0:
```python
import jax
import jax.numpy as jnp
from jax import lax
from jax.sharding import PartitionSpec as P

M = 3


def with_halo(cells, sides, width):
    for axis, dim in sides:
        count = lax.axis_size(axis)
        ends = count - 1
        head = lax.slice_in_dim(cells, 0, width, axis=dim)
        tail = lax.slice_in_dim(cells, cells.shape[dim] - width, cells.shape[dim], axis=dim)
        cells = jnp.concatenate(
            [
                lax.ppermute(tail, axis, [(i, (i + 1) % count) for i in range(ends)]),
                cells,
                lax.ppermute(head, axis, [((i + 1) % count, i) for i in range(ends)]),
            ],
            axis=dim,
        )
    return cells


def shifted(padded, which, sign):
    starts = [1, 1, 1]
    starts[which] = 1 + sign
    limits = [starts[dim] + padded.shape[dim] - 2 for dim in range(3)]
    return lax.slice(padded, starts, limits)


def extend_z(padded):
    return jnp.pad(padded, ((0, 0), (0, 0), (1, 1)))


def stencil(field, kappa_pad):
    padded = extend_z(with_halo(field, (("gx", 0), ("gy", 1)), 1))
    centre = shifted(padded, 0, 0)
    middle = shifted(kappa_pad, 0, 0)
    result = jnp.zeros_like(centre)
    for which in range(3):
        for sign in (-1, 1):
            result = result + 0.5 * (middle + shifted(kappa_pad, which, sign)) * (
                centre - shifted(padded, which, sign)
            )
    return result


def global_norm(vector):
    return jnp.sqrt(lax.psum(jnp.sum(vector * vector), ("gx", "gy")))


def least_squares(columns, beta):
    count = len(columns)
    rhs_vals = [beta] + [jnp.float32(0.0)] * count
    cosines = []
    sines = []
    upper = []
    for column in range(count):
        entries = list(columns[column])
        for earlier in range(column):
            first = entries[earlier]
            second = entries[earlier + 1]
            entries[earlier] = cosines[earlier] * first + sines[earlier] * second
            entries[earlier + 1] = -sines[earlier] * first + cosines[earlier] * second
        first = entries[column]
        second = entries[column + 1]
        radius = jnp.sqrt(first * first + second * second)
        cosines.append(first / radius)
        sines.append(second / radius)
        entries[column] = radius
        rhs_vals[column + 1] = -sines[column] * rhs_vals[column]
        rhs_vals[column] = cosines[column] * rhs_vals[column]
        upper.append(entries[: column + 1])
    coeffs = [None] * count
    for row in reversed(range(count)):
        value = rhs_vals[row]
        for later in range(row + 1, count):
            value = value - upper[later][row] * coeffs[later]
        coeffs[row] = value / upper[row][row]
    return (coeffs, jnp.abs(rhs_vals[count]))


def local(right_side, start_guess, conductivity):
    kappa_pad = extend_z(with_halo(conductivity, (("gx", 0), ("gy", 1)), 1))
    start = right_side - stencil(start_guess, kappa_pad)
    beta = global_norm(start)
    basis = [start / beta]
    columns = []
    for column in range(M):
        vector = stencil(basis[column], kappa_pad)
        local_dots = jnp.stack([jnp.sum(vector * basis[earlier]) for earlier in range(column + 1)])
        coeff_all, squares = lax.psum((local_dots, jnp.sum(vector * vector)), ("gx", "gy"))
        for earlier in range(column + 1):
            vector = vector - coeff_all[earlier] * basis[earlier]
        entries = [coeff_all[earlier] for earlier in range(column + 1)]
        length = jnp.sqrt(squares - jnp.sum(coeff_all * coeff_all))
        entries.append(length)
        columns.append(entries)
        basis.append(vector / length)
    coeffs, estimate = least_squares(columns, beta)
    solution_field = start_guess
    for column in range(M):
        solution_field = solution_field + coeffs[column] * basis[column]
    return (solution_field, estimate)


def solution(mesh):
    in_specs = (P("gx", "gy", None), P("gx", "gy", None), P("gx", "gy", None))
    out_specs = (P("gx", "gy", None), P())
    return jax.shard_map(local, mesh=mesh, in_specs=in_specs, out_specs=out_specs, check_vma=False)
```

profile of v0, /device:TPU:0, one launch (start us, length us, event | category | flops | bytes accessed | tf_op | source)
XLA Modules:
  0.0 344.9 jit_solution(8450779061837298228)
XLA Ops:
  6.3 5.2 %collective-permute-start.1 = (f32[1,32,512]{2,0,1:T(1,128)S(1)}, f32[1,32,512]{2,0,1:T(1,128)S(1)}, u32[]{:S(2)}, u32[]{:S(2)}) collective-permute-start(f32[1,32,512]{2,0,1:T(1,128)S(1)} %copy.8), channel_id=1, source_target_pairs={{0,8},{8,16},{16,24},{1,9},{9,17},{17,25},{2,10},{10,18},{18,26},{... | collective-permute-start | bytes 196616 | tf_op jit(solution)/shard_map/ppermute | solution.py:17
  17.1 3.4 collective-permute-start.4
  21.9 4.6 %collective-permute-start.5 = (f32[34,1,512]{2,0,1:T(8,128)S(1)}, f32[34,1,512]{2,0,1:T(8,128)S(1)}, u32[]{:S(2)}, u32[]{:S(2)}) collective-permute-start(f32[34,1,512]{2,0,1:T(8,128)S(1)} %get-tuple-element.31), channel_id=1, source_target_pairs={{0,1},{1,2},{2,3},{3,4},{4,5},{5,6},{6,7},{8,9},{9,10},{10,11},{11... | collective-permute-start | bytes 208904 | tf_op jit(solution)/shard_map/ppermute | solution.py:17
  27.8 3.1 select_maximum_fusion.16
  33.3 3.0 select_maximum_fusion.12
  36.4 9.9 %multiply_reduce_fusion.9 = (f32[]{:T(128)}, f32[32,32,512]{2,0,1:T(8,128)}) fusion(f32[32,32,512]{2,0,1:T(8,128)S(1)} %copy.28, f32[34,34,514]{2,0,1:T(8,128)S(1)} %select_maximum_fusion.12, f32[32,32,512]{2,0,1:T(8,128)S(1)} %copy.7, f32[34,34,514]{2,0,1:T(8,128)S(1)} %select_maximum_fusion.16, f32[34,1,512]{2,0,1:T(8,128)S(1)} %collective-permute-done.7, ...), kind=kLoop, calls=%fused_computation.156 | loop fusion | flops 25165824 | bytes 17317892 | tf_op jit(solution)/shard_map/reduce_sum | solution.py:51
  46.3 44.5 %psum.49 = f32[]{:T(128)} all-reduce(f32[]{:T(128)} %get-tuple-element.21), channel_id=1, replica_groups=mesh['gx'=4,'gy'=8] {'gx','gy'}, use_global_device_ids=true, to_apply=%region_1.2 | all-reduce | flops 1 | bytes 8 | tf_op jit(solution)/shard_map/psum | solution.py:51
  96.0 4.5 %collective-permute-done.9 = f32[1,32,512]{2,0,1:T(1,128)S(1)} collective-permute-done((f32[1,32,512]{2,0,1:T(1,128)S(1)}, f32[1,32,512]{2,0,1:T(1,128)S(1)}, u32[]{:S(2)}, u32[]{:S(2)}) %collective-permute-start.9) | collective-permute-done | bytes 65568 | tf_op jit(solution)/shard_map/ppermute | solution.py:19
  104.7 4.5 %collective-permute-done.11 = f32[34,1,512]{2,0,1:T(8,128)S(1)} collective-permute-done((f32[34,1,512]{2,0,1:T(8,128)S(1)}, f32[34,1,512]{2,0,1:T(8,128)S(1)}, u32[]{:S(2)}, u32[]{:S(2)}) %collective-permute-start.11) | collective-permute-done | bytes 69664 | tf_op jit(solution)/shard_map/ppermute | solution.py:19
  109.1 3.0 select_maximum_fusion.8
  112.2 8.3 %multiply_reduce_fusion.8 = (f32[]{:T(128)}, f32[]{:T(128)}, f32[32,32,512]{2,0,1:T(8,128)}) fusion(f32[32,32,512]{2,0,1:T(8,128)S(1)} %broadcast_divide_fusion, f32[34,34,514]{2,0,1:T(8,128)S(1)} %select_maximum_fusion.8, f32[32,32,512]{2,0,1:T(8,128)S(1)} %copy-done.5, f32[34,34,514]{2,0,1:T(8,128)S(1)} %select_maximum_fusion.16, ...), kind=kLoop, calls=%fused_computation.155 | loop fusion | flops 25690112 | bytes 15220744 | tf_op jit(solution)/shard_map/reduce_sum | solution.py:93
  120.5 42.9 %all-reduce.7 = (f32[]{:T(128)}, f32[1]{0:T(128)}) all-reduce(f32[]{:T(128)} %get-tuple-element.12, f32[1]{0:T(128)} %bitcast), channel_id=1, replica_groups=mesh['gx'=4,'gy'=8] {'gx','gy'}, use_global_device_ids=true, to_apply=%region_5.6 | all-reduce | flops 2 | bytes 16 | tf_op jit(solution)/shard_map/psum | solution.py:94
  165.4 3.4 subtract_divide_fusion.1
  171.5 4.6 %collective-permute-done.13 = f32[1,32,512]{2,0,1:T(1,128)S(1)} collective-permute-done((f32[1,32,512]{2,0,1:T(1,128)S(1)}, f32[1,32,512]{2,0,1:T(1,128)S(1)}, u32[]{:S(2)}, u32[]{:S(2)}) %collective-permute-start.13) | collective-permute-done | bytes 65568 | tf_op jit(solution)/shard_map/ppermute | solution.py:19
  180.2 4.6 %collective-permute-done.15 = f32[34,1,512]{2,0,1:T(8,128)S(1)} collective-permute-done((f32[34,1,512]{2,0,1:T(8,128)S(1)}, f32[34,1,512]{2,0,1:T(8,128)S(1)}, u32[]{:S(2)}, u32[]{:S(2)}) %collective-permute-start.15) | collective-permute-done | bytes 69664 | tf_op jit(solution)/shard_map/ppermute | solution.py:19
  184.8 3.0 select_maximum_fusion.4
  187.9 8.6 %multiply_reduce_fusion.6 = (f32[]{:T(128)}, f32[]{:T(128)}, f32[]{:T(128)}, f32[32,32,512]{2,0,1:T(8,128)}) fusion(f32[32,32,512]{2,0,1:T(8,128)S(1)} %subtract_divide_fusion.1, f32[34,34,514]{2,0,1:T(8,128)S(1)} %select_maximum_fusion.4, f32[32,32,512]{2,0,1:T(8,128)S(1)} %copy-done.6, f32[34,34,514]{2,0,1:T(8,128)S(1)} %select_maximum_fusion.16, ...), kind=kLoop, calls=%fused_computation.152 | loop fusion | flops 27262976 | bytes 17317904 | tf_op jit(solution)/shard_map/reduce_sum | solution.py:93
  197.9 42.9 %all-reduce.6 = (f32[]{:T(128)}, f32[2]{0:T(128)S(1)}) all-reduce(f32[]{:T(128)} %get-tuple-element.9, f32[2]{0:T(128)S(1)} %pad_maximum_fusion.55), channel_id=1, replica_groups=mesh['gx'=4,'gy'=8] {'gx','gy'}, use_global_device_ids=true, to_apply=%region_10.11 | all-reduce | flops 3 | bytes 24 | tf_op jit(solution)/shard_map/psum | solution.py:94
  243.6 5.0 %subtract_divide_fusion = f32[32,32,512]{2,0,1:T(8,128)S(1)} fusion(f32[32,32,512]{2,0,1:T(8,128)} %copy-done, f32[32,32,512]{2,0,1:T(8,128)} %get-tuple-element.19, f32[]{:T(128)S(6)} %sqrt.24, f32[]{:T(128)} %bitcast.6, f32[]{:T(128)} %bitcast.5, f32[32,32,512]{2,0,1:T(8,128)} %get-tuple-element.22, f32[]{:T(128)S(6)} %sqrt.21), kind=kLoop, calls=%fused_computation.149 | loop fusion | flops 3145728 | bytes 8388624 | tf_op jit(solution)/shard_map/div | solution.py:101
  251.3 4.6 %collective-permute-done.17 = f32[1,32,512]{2,0,1:T(1,128)S(1)} collective-permute-done((f32[1,32,512]{2,0,1:T(1,128)S(1)}, f32[1,32,512]{2,0,1:T(1,128)S(1)}, u32[]{:S(2)}, u32[]{:S(2)}) %collective-permute-start.17) | collective-permute-done | bytes 65568 | tf_op jit(solution)/shard_map/ppermute | solution.py:19
  265.9 4.6 %select_maximum_fusion = f32[34,34,514]{2,0,1:T(8,128)S(1)} fusion(f32[34,1,512]{2,0,1:T(8,128)} %collective-permute-done.19, f32[34,1,512]{2,0,1:T(8,128)} %collective-permute-done.18, f32[1,32,512]{2,0,1:T(1,128)} %copy-done.24, f32[32,32,512]{2,0,1:T(8,128)} %copy-done.7, f32[1,32,512]{2,0,1:T(1,128)} %copy-done.22), kind=kLoop, calls=%fused_computation.2 | loop fusion | flops 7130208 | bytes 4744224 | tf_op jit(solution)/shard_map/concatenate | solution.py:15
  270.5 14.5 %multiply_reduce_fusion = (f32[]{:T(128)}, f32[]{:T(128)}, f32[]{:T(128)}, f32[]{:T(128)}) fusion(f32[32,32,512]{2,0,1:T(8,128)} %copy-done.7, f32[32,32,512]{2,0,1:T(8,128)S(1)} %copy-done.1, f32[34,34,514]{2,0,1:T(8,128)S(1)} %select_maximum_fusion, f32[32,32,512]{2,0,1:T(8,128)} %copy-done.4, f32[34,34,514]{2,0,1:T(8,128)S(1)} %select_maximum_fusion.16, ...), kind=kLoop, calls=%fused_computation.145 | loop fusion | flops 28311552 | bytes 17317908 | tf_op jit(solution)/shard_map/reduce_sum | solution.py:94
  286.9 42.5 %all-reduce.5 = (f32[3]{0:T(128)S(1)}, f32[]{:T(128)}) all-reduce(f32[3]{0:T(128)S(1)} %pad_maximum_fusion.56, f32[]{:T(128)} %get-tuple-element.4), channel_id=1, replica_groups=mesh['gx'=4,'gy'=8] {'gx','gy'}, use_global_device_ids=true, to_apply=%region_15.16 | all-reduce | flops 4 | bytes 32 | tf_op jit(solution)/shard_map/psum | solution.py:94
  335.9 5.4 %multiply_add_fusion = f32[32,32,512]{2,0,1:T(8,128)S(1)} fusion(f32[32,32,512]{2,0,1:T(8,128)} %copy-done.7, f32[32,32,512]{2,0,1:T(8,128)} %copy-done, f32[]{:T(128)S(6)} %div.56, f32[]{:T(128)S(6)} %div.57, f32[]{:T(128)S(6)} %div.58, f32[32,32,512]{2,1,0:T(8,128)} %param.4, f32[32,32,512]{2,0,1:T(8,128)} %get-tuple-element.22, f32[]{:T(128)S(6)} %sqrt.21), kind=kLoop, calls=%fused_computation.144 | loop fusion | flops 3670016 | bytes 10485776 | tf_op jit(solution)/shard_map/add | solution.py:105
  (108 shorter events, 47.9 us)
Async XLA Ops:
  1.6 15.5 %collective-permute-start = (f32[1,32,512]{2,0,1:T(1,128)S(1)}, f32[1,32,512]{2,0,1:T(1,128)S(1)}, u32[]{:S(2)}, u32[]{:S(2)}) collective-permute-start(f32[1,32,512]{2,0,1:T(1,128)S(1)} %copy.5), channel_id=1, source_target_pairs={{0,8},{8,16},{16,24},{1,9},{9,17},{17,25},{2,10},{10,18},{18,26},{... | collective-permute-start | bytes 196616 | tf_op jit(solution)/shard_map/ppermute | solution.py:17
  4.1 13.0 %collective-permute-start.2 = (f32[1,32,512]{2,0,1:T(1,128)S(1)}, f32[1,32,512]{2,0,1:T(1,128)S(1)}, u32[]{:S(2)}, u32[]{:S(2)}) collective-permute-start(f32[1,32,512]{2,0,1:T(1,128)S(1)} %copy.11), channel_id=1, source_target_pairs={{8,0},{16,8},{24,16},{9,1},{17,9},{25,17},{10,2},{18,10},{26,18},{... | collective-permute-start | bytes 196616 | tf_op jit(solution)/shard_map/ppermute | solution.py:19
  6.3 15.5 %collective-permute-start.1 = (f32[1,32,512]{2,0,1:T(1,128)S(1)}, f32[1,32,512]{2,0,1:T(1,128)S(1)}, u32[]{:S(2)}, u32[]{:S(2)}) collective-permute-start(f32[1,32,512]{2,0,1:T(1,128)S(1)} %copy.8), channel_id=1, source_target_pairs={{0,8},{8,16},{16,24},{1,9},{9,17},{17,25},{2,10},{10,18},{18,26},{... | collective-permute-start | bytes 196616 | tf_op jit(solution)/shard_map/ppermute | solution.py:17
  11.6 10.3 %collective-permute-start.3 = (f32[1,32,512]{2,0,1:T(1,128)S(1)}, f32[1,32,512]{2,0,1:T(1,128)S(1)}, u32[]{:S(2)}, u32[]{:S(2)}) collective-permute-start(f32[1,32,512]{2,0,1:T(1,128)S(1)} %copy.14), channel_id=1, source_target_pairs={{8,0},{16,8},{24,16},{9,1},{17,9},{25,17},{10,2},{18,10},{26,18},{... | collective-permute-start | bytes 196616 | tf_op jit(solution)/shard_map/ppermute | solution.py:19
  15.8 20.5 %copy-start.4 = (f32[32,32,512]{2,0,1:T(8,128)}, f32[32,32,512]{2,0,1:T(8,128)S(1)}, u32[]{:S(2)}) copy-start(f32[32,32,512]{2,0,1:T(8,128)S(1)} %copy.7) | copy-start | bytes 6291460
  17.1 19.2 %copy-start.9 = (f32[1,32,512]{2,0,1:T(1,128)}, f32[1,32,512]{2,0,1:T(1,128)S(1)}, u32[]{:S(2)}) copy-start(f32[1,32,512]{2,0,1:T(1,128)S(1)} %collective-permute-done.2) | copy-start | bytes 196612
  17.1 10.6 %collective-permute-start.4 = (f32[34,1,512]{2,0,1:T(8,128)S(1)}, f32[34,1,512]{2,0,1:T(8,128)S(1)}, u32[]{:S(2)}, u32[]{:S(2)}) collective-permute-start(f32[34,1,512]{2,0,1:T(8,128)S(1)} %get-tuple-element.29), channel_id=1, source_target_pairs={{0,1},{1,2},{2,3},{3,4},{4,5},{5,6},{6,7},{8,9},{9,10},{10,11},{11... | collective-permute-start | bytes 208904 | tf_op jit(solution)/shard_map/ppermute | solution.py:17
  20.6 7.2 %collective-permute-start.6 = (f32[34,1,512]{2,0,1:T(8,128)S(1)}, f32[34,1,512]{2,0,1:T(8,128)S(1)}, u32[]{:S(2)}, u32[]{:S(2)}) collective-permute-start(f32[34,1,512]{2,0,1:T(8,128)S(1)} %get-tuple-element.30), channel_id=1, source_target_pairs={{1,0},{2,1},{3,2},{4,3},{5,4},{6,5},{7,6},{9,8},{10,9},{11,10},{12... | collective-permute-start | bytes 208904 | tf_op jit(solution)/shard_map/ppermute | solution.py:19
  21.9 9.0 %collective-permute-start.5 = (f32[34,1,512]{2,0,1:T(8,128)S(1)}, f32[34,1,512]{2,0,1:T(8,128)S(1)}, u32[]{:S(2)}, u32[]{:S(2)}) collective-permute-start(f32[34,1,512]{2,0,1:T(8,128)S(1)} %get-tuple-element.31), channel_id=1, source_target_pairs={{0,1},{1,2},{2,3},{3,4},{4,5},{5,6},{6,7},{8,9},{9,10},{10,11},{11... | collective-permute-start | bytes 208904 | tf_op jit(solution)/shard_map/ppermute | solution.py:17
  26.5 6.8 %collective-permute-start.7 = (f32[34,1,512]{2,0,1:T(8,128)S(1)}, f32[34,1,512]{2,0,1:T(8,128)S(1)}, u32[]{:S(2)}, u32[]{:S(2)}) collective-permute-start(f32[34,1,512]{2,0,1:T(8,128)S(1)} %get-tuple-element.32), channel_id=1, source_target_pairs={{1,0},{2,1},{3,2},{4,3},{5,4},{6,5},{7,6},{9,8},{10,9},{11,10},{12... | collective-permute-start | bytes 208904 | tf_op jit(solution)/shard_map/ppermute | solution.py:19
  93.4 2.6 collective-permute-start.8
  94.7 5.8 %collective-permute-start.9 = (f32[1,32,512]{2,0,1:T(1,128)S(1)}, f32[1,32,512]{2,0,1:T(1,128)S(1)}, u32[]{:S(2)}, u32[]{:S(2)}) collective-permute-start(f32[1,32,512]{2,0,1:T(1,128)S(1)} %get-tuple-element.38), channel_id=1, source_target_pairs={{8,0},{16,8},{24,16},{9,1},{17,9},{25,17},{10,2},{18,10},{26,18},{... | collective-permute-start | bytes 196616 | tf_op jit(solution)/shard_map/ppermute | solution.py:19
  100.6 4.1 %collective-permute-start.10 = (f32[34,1,512]{2,0,1:T(8,128)S(1)}, f32[34,1,512]{2,0,1:T(8,128)S(1)}, u32[]{:S(2)}, u32[]{:S(2)}) collective-permute-start(f32[34,1,512]{2,0,1:T(8,128)S(1)} %get-tuple-element.27), channel_id=1, source_target_pairs={{0,1},{1,2},{2,3},{3,4},{4,5},{5,6},{6,7},{8,9},{9,10},{10,11},{11... | collective-permute-start | bytes 208904 | tf_op jit(solution)/shard_map/ppermute | solution.py:17
  102.7 6.5 %collective-permute-start.11 = (f32[34,1,512]{2,0,1:T(8,128)S(1)}, f32[34,1,512]{2,0,1:T(8,128)S(1)}, u32[]{:S(2)}, u32[]{:S(2)}) collective-permute-start(f32[34,1,512]{2,0,1:T(8,128)S(1)} %get-tuple-element.28), channel_id=1, source_target_pairs={{1,0},{2,1},{3,2},{4,3},{5,4},{6,5},{7,6},{9,8},{10,9},{11,10},{12... | collective-permute-start | bytes 208904 | tf_op jit(solution)/shard_map/ppermute | solution.py:19
  168.8 19.0 %copy-start = (f32[32,32,512]{2,0,1:T(8,128)}, f32[32,32,512]{2,0,1:T(8,128)S(1)}, u32[]{:S(2)}) copy-start(f32[32,32,512]{2,0,1:T(8,128)S(1)} %subtract_divide_fusion.1) | copy-start | bytes 6291460
  168.9 2.6 collective-permute-start.12
  170.2 5.9 %collective-permute-start.13 = (f32[1,32,512]{2,0,1:T(1,128)S(1)}, f32[1,32,512]{2,0,1:T(1,128)S(1)}, u32[]{:S(2)}, u32[]{:S(2)}) collective-permute-start(f32[1,32,512]{2,0,1:T(1,128)S(1)} %get-tuple-element.36), channel_id=1, source_target_pairs={{8,0},{16,8},{24,16},{9,1},{17,9},{25,17},{10,2},{18,10},{26,18},{... | collective-permute-start | bytes 196616 | tf_op jit(solution)/shard_map/ppermute | solution.py:19
  176.2 4.0 %collective-permute-start.14 = (f32[34,1,512]{2,0,1:T(8,128)S(1)}, f32[34,1,512]{2,0,1:T(8,128)S(1)}, u32[]{:S(2)}, u32[]{:S(2)}) collective-permute-start(f32[34,1,512]{2,0,1:T(8,128)S(1)} %get-tuple-element.25), channel_id=1, source_target_pairs={{0,1},{1,2},{2,3},{3,4},{4,5},{5,6},{6,7},{8,9},{9,10},{10,11},{11... | collective-permute-start | bytes 208904 | tf_op jit(solution)/shard_map/ppermute | solution.py:17
  178.2 9.7 %copy-start.2 = (f32[32,32,512]{2,0,1:T(8,128)S(1)}, f32[32,32,512]{2,0,1:T(8,128)}, u32[]{:S(2)}) copy-start(f32[32,32,512]{2,0,1:T(8,128)} %get-tuple-element.22) | copy-start | bytes 6291460
  178.2 6.6 %collective-permute-start.15 = (f32[34,1,512]{2,0,1:T(8,128)S(1)}, f32[34,1,512]{2,0,1:T(8,128)S(1)}, u32[]{:S(2)}, u32[]{:S(2)}) collective-permute-start(f32[34,1,512]{2,0,1:T(8,128)S(1)} %get-tuple-element.26), channel_id=1, source_target_pairs={{1,0},{2,1},{3,2},{4,3},{5,4},{6,5},{7,6},{9,8},{10,9},{11,10},{12... | collective-permute-start | bytes 208904 | tf_op jit(solution)/shard_map/ppermute | solution.py:19
  248.7 2.6 collective-permute-start.16
  250.0 5.9 %collective-permute-start.17 = (f32[1,32,512]{2,0,1:T(1,128)S(1)}, f32[1,32,512]{2,0,1:T(1,128)S(1)}, u32[]{:S(2)}, u32[]{:S(2)}) collective-permute-start(f32[1,32,512]{2,0,1:T(1,128)S(1)} %get-tuple-element.34), channel_id=1, source_target_pairs={{8,0},{16,8},{24,16},{9,1},{17,9},{25,17},{10,2},{18,10},{26,18},{... | collective-permute-start | bytes 196616 | tf_op jit(solution)/shard_map/ppermute | solution.py:19
  256.6 9.0 %collective-permute-start.18 = (f32[34,1,512]{2,0,1:T(8,128)}, f32[34,1,512]{2,0,1:T(8,128)}, u32[]{:S(2)}, u32[]{:S(2)}) collective-permute-start(f32[34,1,512]{2,0,1:T(8,128)} %get-tuple-element.23), channel_id=1, source_target_pairs={{0,1},{1,2},{2,3},{3,4},{4,5},{5,6},{6,7},{8,9},{9,10},{10,11},{11... | collective-permute-start | bytes 208904 | tf_op jit(solution)/shard_map/ppermute | solution.py:17
  259.2 6.6 %collective-permute-start.19 = (f32[34,1,512]{2,0,1:T(8,128)}, f32[34,1,512]{2,0,1:T(8,128)}, u32[]{:S(2)}, u32[]{:S(2)}) collective-permute-start(f32[34,1,512]{2,0,1:T(8,128)} %get-tuple-element.24), channel_id=1, source_target_pairs={{1,0},{2,1},{3,2},{4,3},{5,4},{6,5},{7,6},{9,8},{10,9},{11,10},{12... | collective-permute-start | bytes 208904 | tf_op jit(solution)/shard_map/ppermute | solution.py:19
  (22 other events, 151.9 us)
where the time goes:
time: 347 us; the launch traced here: 345 us
  blocking collectives  173 us (50%)
  other arithmetic  79 us (23%)
  starting transfers between devices  39.9 us (11%)
  waiting for transfers between devices  26.3 us (8%)
  between operations  16.7 us (5%)
  local copies, waits for them, and re-layouts  10.4 us (3%)
    psum x3, blocking collectives, local(): lax.psum((local_dots, jnp.sum(vector * vector)), ('gx', 'gy'))  128 us
    psum x1, blocking collectives, global_norm(): return jnp.sqrt(lax.psum(jnp.sum(vector * vector), ('gx', 'gy')))  44.5 us
    ppermute x10, starting transfers between devices, with_halo(): lax.ppermute(tail, axis, [(i, (i + 1) % count) for i in range(ends)])  26 us
    ppermute x10, waiting for transfers between devices, with_halo(): lax.ppermute(head, axis, [((i + 1) % count, i) for i in range(ends)])  25.5 us
    reduce_sum x2, other arithmetic, local(): jnp.sum(vector * basis[earlier])  16.9 us
    concatenate x5, other arithmetic, with_halo(): jnp.concatenate([lax.ppermute(tail, axis, [(i, (i + 1) % count) for i in...  16.7 us
    reduce_sum x1, other arithmetic, local(): jnp.sum(vector * vector)  14.5 us
    ppermute x10, starting transfers between devices, with_halo(): lax.ppermute(head, axis, [((i + 1) % count, i) for i in range(ends)])  13.8 us
  transfers between devices with their start and end apart: 20, of which 9 were waited for; matrix products, arithmetic and copies ran while one was open for 2% of the time, Pallas kernels for 0%

commit v1 on v0

v1 whole, which is shorter than its diff:
```python
import functools

import jax
import jax.numpy as jnp
from jax import lax
from jax.experimental import pallas as pl
from jax.experimental.pallas import tpu as pltpu
from jax.sharding import PartitionSpec as P

M = 3
SCALE = 128.0
SMALL = 2.0**-14
VMEM_SPEC = pl.BlockSpec(memory_space=pltpu.VMEM)
ANY_SPEC = pl.BlockSpec(memory_space=pl.ANY)
F32 = jnp.float32


def vmem(shape):
    return pltpu.VMEM(shape, F32)


def call(body, out_shape, n_in, flops=0, scratch=(), aliases=None, any_in=(), any_out=(), name=None):
    outs = list(out_shape)
    return pl.pallas_call(
        body,
        out_shape=outs,
        in_specs=[ANY_SPEC if i in any_in else VMEM_SPEC for i in range(n_in)],
        out_specs=[ANY_SPEC if i in any_out else VMEM_SPEC for i in range(len(outs))],
        scratch_shapes=list(scratch),
        input_output_aliases=aliases or {},
        cost_estimate=pl.CostEstimate(flops=flops, bytes_accessed=0, transcendentals=0),
        compiler_params=pltpu.CompilerParams(vmem_limit_bytes=16 * 1024 * 1024),
        name=name,
    )


def pairings(sizes):
    nx, ny = sizes
    at = lambda i, j: i * ny + j
    ends = lambda i, n: i == 0 or i == n - 1
    gx_a, gx_b, gy_a, gy_b = [], [], [], []
    for i in range(nx):
        for j in range(ny):
            gx_a.append((at(i, j), at(i ^ 1, j)))
            gy_a.append((at(i, j), at(i, j ^ 1)))
            gx_b.append((at(i, j), at(nx - 1 - i if ends(i, nx) else ((i + 1) ^ 1) - 1, j)))
            gy_b.append((at(i, j), at(i ^ 1, j) if ends(j, ny) else at(i, ((j + 1) ^ 1) - 1)))
    return gx_a, gx_b, gy_a, gy_b


def exchange(parts, sizes):
    moved = [lax.ppermute(part, ("gx", "gy"), pairs) for part, pairs in zip(parts, pairings(sizes))]
    return moved


def sides(sizes, shape):
    out = []
    for name, count, rows in (("gx", sizes[0], shape[0]), ("gy", sizes[1], shape[1])):
        index = lax.axis_index(name)
        odd = lax.rem(index, 2)
        inside = jnp.logical_and(index > 0, index < count - 1)
        out.append(((1 - odd) * (rows - 1), odd * (rows - 1), inside))
    return out


def faces_kernel(sizes, x_hbm, k_hbm, x_ref, k_ref, xa, xb, ya, yb, sem):
    copies = [pltpu.make_async_copy(k_hbm, k_ref, sem.at[0]), pltpu.make_async_copy(x_hbm, x_ref, sem.at[1])]
    for copy in copies:
        copy.start()
    (ax, bx, _), (ay, by, _) = sides(sizes, x_ref.shape)
    for copy in copies:
        copy.wait()
    for at, ref in enumerate((x_ref, k_ref)):
        xa[at] = ref[ax]
        xb[at] = ref[bx]
        for row in range(ref.shape[0]):
            ya[at, pl.ds(row, 1)] = ref[row, pl.ds(ay, 1)]
            yb[at, pl.ds(row, 1)] = ref[row, pl.ds(by, 1)]


def tree(parts):
    while len(parts) > 1:
        parts = [parts[i] + parts[i + 1] if i + 1 < len(parts) else parts[i] for i in range(0, len(parts), 2)]
    return parts[0]


def folded(plane):
    rows, lanes = plane.shape
    return tree([plane[r : r + 8, c : c + 128] for r in range(0, rows, 8) for c in range(0, lanes, 128)])


def applied(u_ref, x, cx_lo, cx_hi, cy, cz, end):
    last = u_ref.shape[0] - 1
    rows, lanes = u_ref.shape[1:]
    u = u_ref[x]
    w = cx_hi * (u - u_ref[jnp.minimum(x + 1, last)]) + cx_lo * (u - u_ref[jnp.maximum(x - 1, 0)])
    flux = cy * (u - pltpu.roll(u, rows - 1, 0))
    w = w + (flux - pltpu.roll(flux, 1, 0))
    flux = cz * (u - pltpu.roll(u, lanes - 1, 1))
    return u, w + (flux - pltpu.roll(flux, 1, 1)) + end * u


def start_kernel(x_ref, k_ref, b_hbm, r_ref, cx_ref, cy_ref, cz_ref, end_ref, b_ref, sem):
    planes, rows, lanes = x_ref.shape
    step = 8
    copies = [
        pltpu.make_async_copy(b_hbm.at[pl.ds(p, step)], b_ref.at[pl.ds(p, step)], sem.at[p // step])
        for p in range(0, planes, step)
    ]
    for copy in copies:
        copy.start()
    row = lax.broadcasted_iota(jnp.int32, (rows, lanes), 0)
    lane = lax.broadcasted_iota(jnp.int32, (rows, lanes), 1)
    half = 0.5 / SCALE
    cx_ref[0] = jnp.zeros((rows, lanes), F32)

    def plane(x, carry):
        k = k_ref[x]
        above = k_ref[jnp.minimum(x + 1, planes - 1)]
        cx_hi = jnp.where(x == planes - 1, 0.0, half * (k + above))
        cy = jnp.where(row == rows - 1, 0.0, half * (k + pltpu.roll(k, rows - 1, 0)))
        cz = jnp.where(lane == lanes - 1, 0.0, half * (k + pltpu.roll(k, lanes - 1, 1)))
        end = jnp.where(jnp.logical_or(lane == 0, lane == lanes - 1), half * k, 0.0)
        cx_ref[x + 1] = cx_hi
        cy_ref[x] = cy
        cz_ref[x] = cz
        end_ref[x] = end
        _, w = applied(x_ref, x, cx_ref[x], cx_hi, cy, cz, end)
        r_ref[x] = b_ref[x] - SCALE * w
        return carry

    for at, copy in enumerate(copies):
        copy.wait()
        lax.fori_loop(at * step, (at + 1) * step, plane, 0)


def apply_kernel(with_older, last, *refs):
    u_ref, cx_ref, cy_ref, cz_ref, end_ref = refs[:5]
    older_ref = refs[5] if with_older else None
    w_ref, dots_ref = refs[-2:]
    planes = u_ref.shape[0]

    def plane(x, sums):
        u, w = applied(u_ref, x, cx_ref[x], cx_ref[x + 1], cy_ref[x], cz_ref[x], end_ref[x])
        w_ref[x] = w
        terms = [u * u]
        if with_older:
            terms.append(u * older_ref[x])
        if last:
            terms += [u * w, w * w]
        return tuple(s + folded(t) for s, t in zip(sums, terms))

    count = 1 + with_older + 2 * last
    sums = lax.fori_loop(0, planes, plane, tuple(jnp.zeros((8, 128), F32) for _ in range(count)))
    for at, s in enumerate(sums):
        dots_ref[at] = s


def start_fix_kernel(sizes, r_in, sxa, sxb, sya, syb, hxa, hxb, hya, hyb, r_ref, cxa, cxb, cya, cyb, oxa, oxb, oya, oyb):
    (ax, bx, in_x), (ay, by, in_y) = sides(sizes, r_ref.shape)
    half = 0.5 / SCALE

    def terms(sent, halo, inside):
        field, k = halo[0], halo[1]
        if inside is not None:
            field, k = jnp.where(inside, field, 0.0), jnp.where(inside, k, 0.0)
        c = half * (sent[1] + k)
        return c, SCALE * (c * (sent[0] - field))

    cxa[...], dxa = terms(sxa, hxa, None)
    cxb[...], dxb = terms(sxb, hxb, in_x)
    cya[...], dya = terms(sya, hya, None)
    cyb[...], dyb = terms(syb, hyb, in_y)
    r_ref[ax] = r_ref[ax] - dxa
    r_ref[bx] = r_ref[bx] - dxb
    for row in range(r_ref.shape[0]):
        for at, d, out in ((ay, dya, oya), (by, dyb, oyb)):
            new = r_ref[row, pl.ds(at, 1)] - d[row : row + 1]
            r_ref[row, pl.ds(at, 1)] = new
            out[pl.ds(row, 1)] = new
    oxa[...] = r_ref[ax]
    oxb[...] = r_ref[bx]


def fix_terms(sizes, shape, sends, halos, coeffs):
    (ax, bx, in_x), (ay, by, in_y) = sides(sizes, shape)
    out = []
    for sent, halo, c, inside in zip(sends, halos, coeffs, (None, in_x, None, in_y)):
        field = halo[...]
        if inside is not None:
            field = jnp.where(inside, field, 0.0)
        out.append(c[...] * (sent[...] - field))
    return (ax, bx, ay, by), out


def fix_kernel(sizes, w_in, *refs):
    sends, halos, coeffs, (w_ref, oxa, oxb, oya, oyb) = refs[:4], refs[4:8], refs[8:12], refs[12:]
    (ax, bx, ay, by), (dxa, dxb, dya, dyb) = fix_terms(sizes, w_ref.shape, sends, halos, coeffs)
    w_ref[ax] = w_ref[ax] + dxa
    w_ref[bx] = w_ref[bx] + dxb
    for row in range(w_ref.shape[0]):
        for at, d, out in ((ay, dya, oya), (by, dyb, oyb)):
            new = w_ref[row, pl.ds(at, 1)] + d[row : row + 1]
            w_ref[row, pl.ds(at, 1)] = new
            out[pl.ds(row, 1)] = new
    oxa[...] = w_ref[ax]
    oxb[...] = w_ref[bx]


def two_sum(a, b):
    s = a + b
    t = s - a
    return s, (a - (s - t)) + (b - t)


def split(a):
    t = 4097.0 * a
    high = t - (t - a)
    return high, a - high


def two_product(a, b):
    p = a * b
    ah, al = split(a)
    bh, bl = split(b)
    return p, ((ah * bh - p) + ah * bl + al * bh) + al * bl


def minus_product(value, factor, other):
    p, e = two_product(factor, other[0])
    s, t = two_sum(value[0], -p)
    t = t + ((value[1] - e) - factor * other[1])
    high = s + t
    return high, t - (high - s)


def folds(high, low, axis):
    shift = high.shape[axis] // 2
    while shift:
        high, err = two_sum(high, pltpu.roll(high, shift, axis))
        low = low + pltpu.roll(low, shift, axis) + err
        shift //= 2
    return high, low


def last_fix_kernel(sizes, w_in, *refs):
    sends, halos, coeffs = refs[:4], refs[4:8], refs[8:12]
    dots0, dots1, dots2, w_ref, out_ref = refs[12:]
    (ax, bx, ay, by), (dxa, dxb, dya, dyb) = fix_terms(sizes, w_ref.shape, sends, halos, coeffs)
    cross, square = [], []
    for at, d, sent in ((ax, dxa, sends[0]), (bx, dxb, sends[1])):
        old = w_ref[at]
        w_ref[at] = old + d
        cross.append(folded(d * sent[...]))
        square.append(folded(d * (old + old + d)))
    for at, d, sent in ((ay, dya, sends[2]), (by, dyb, sends[3])):
        old = jnp.concatenate([w_ref[row, pl.ds(at, 1)] for row in range(w_ref.shape[0])], axis=0)
        cross.append(folded(d * sent[...]))
        square.append(folded(d * (old + old + d)))
    zero = jnp.zeros((8, 128), F32)
    m5 = two_sum(dots2[2], tree(cross))
    m6 = two_sum(dots2[3], tree(square))
    moments = [(dots0[0], zero), (dots1[1], zero), (dots1[0], zero), (dots2[1], zero), (dots2[0], zero), m5, m6]
    sub = lax.broadcasted_iota(jnp.int32, (8, 128), 0)
    lane = lax.broadcasted_iota(jnp.int32, (8, 128), 1)
    high, low = zero, zero
    for at, (h, l) in enumerate(moments):
        h, l = folds(h, l, 0)
        high = jnp.where(sub == at, h, high)
        low = jnp.where(sub == at, l, low)
    high, low = folds(high, low, 1)
    flat = jnp.where(lane == sub, high, jnp.where(lane == sub + 8, low, 0.0))
    for shift in (4, 2, 1):
        flat = flat + pltpu.roll(flat, shift, 0)
    for at in range(out_ref.shape[0]):
        out_ref[at] = flat[0:1]


def least_squares(alphas, offs):
    one = jnp.ones_like(alphas[0])
    rhs = [one] + [jnp.zeros_like(one)] * M
    cosines, sines, upper = [], [], []
    for column in range(M):
        entries = [jnp.zeros_like(one)] * (column + 2)
        if column:
            entries[column - 1] = offs[column - 1]
        entries[column] = alphas[column]
        entries[column + 1] = offs[column]
        for earlier in range(column):
            first, second = entries[earlier], entries[earlier + 1]
            entries[earlier] = cosines[earlier] * first + sines[earlier] * second
            entries[earlier + 1] = cosines[earlier] * second - sines[earlier] * first
        first, second = entries[column], entries[column + 1]
        radius = jnp.sqrt(first * first + second * second)
        cosines.append(first / radius)
        sines.append(second / radius)
        entries[column] = radius
        rhs[column + 1] = -sines[column] * rhs[column]
        rhs[column] = cosines[column] * rhs[column]
        upper.append(entries[: column + 1])
    coeffs = [None] * M
    for row in reversed(range(M)):
        value = rhs[row]
        for later in range(row + 1, M):
            value = value - upper[later][row] * coeffs[later]
        coeffs[row] = value / upper[row][row]
    return coeffs, jnp.abs(rhs[M])


def finish_kernel(sums_ref, x_ref, r_ref, w1_ref, w2_ref, out_hbm, est_ref, out_ref, sem):
    parts = [(sums_ref[at] * SMALL, jnp.zeros((1, 128), F32)) for at in range(sums_ref.shape[0])]
    while len(parts) > 1:
        joined = []
        for at in range(0, len(parts) - 1, 2):
            s, e = two_sum(parts[at][0], parts[at + 1][0])
            joined.append((s, parts[at][1] + parts[at + 1][1] + e))
        parts = joined + parts[len(joined) * 2 :]
    high, low = parts[0]
    lane = lax.broadcasted_iota(jnp.int32, (1, 128), 1)
    pick = lambda row, at: jnp.sum(jnp.where(lane == at, row, 0.0), axis=1, keepdims=True)
    spread = lambda v: jnp.broadcast_to(v, (8, 128))
    m = [
        two_sum(spread(pick(high, at)), spread(pick(low, at) + pick(high, at + 8) + pick(low, at + 8)))
        for at in range(2 * M + 1)
    ]
    older, now = [None] * len(m), m
    ratio = m[1][0] / m[0][0]
    alphas, betas = [ratio], []
    previous = ratio
    for step in range(1, M + 1):
        new = [None] * len(m)
        for at in range(step, len(m) - step):
            value = minus_product(now[at + 1], alphas[step - 1], now[at])
            if step > 1:
                value = minus_product(value, betas[step - 2], older[at])
            new[at] = value
        betas.append(new[step][0] / now[step - 1][0])
        if step < M:
            ratio = new[step + 1][0] / new[step][0]
            alphas.append(ratio - previous)
            previous = ratio
        older, now = now, new
    offs = [jnp.sqrt(b) for b in betas]
    (y0, y1, y2), estimate = least_squares(alphas, offs)
    estimate = estimate * jnp.sqrt(m[0][0]) * (SMALL**-0.5)
    e1 = y1 / offs[0]
    e2 = y2 / (offs[0] * offs[1])
    c0 = (y0 - e1 * alphas[0] + e2 * (alphas[0] * alphas[1] - betas[0])) * (1.0 / SCALE)
    c1 = (e1 - e2 * (alphas[0] + alphas[1])) * (1.0 / SCALE)
    c2 = e2 * (1.0 / SCALE)
    est_ref[...] = estimate[0:1]
    planes, rows, lanes = x_ref.shape
    c0, c1, c2 = (jnp.broadcast_to(c[0:1, 0:1], (rows, lanes)) for c in (c0, c1, c2))
    step = 8

    def plane(x, carry):
        out_ref[x] = x_ref[x] + (c0 * r_ref[x] + c1 * w1_ref[x] + c2 * w2_ref[x])
        return carry

    copies = []
    for p in range(0, planes, step):
        lax.fori_loop(p, p + step, plane, 0)
        copy = pltpu.make_async_copy(out_ref.at[pl.ds(p, step)], out_hbm.at[pl.ds(p, step)], sem.at[p // step])
        copy.start()
        copies.append(copy)
    for copy in copies:
        copy.wait()


def local(sizes, right_side, start_guess, conductivity):
    shape = start_guess.shape
    planes, rows, lanes = shape
    devices = sizes[0] * sizes[1]
    block = vmem(shape)
    x_face, y_face = vmem((rows, lanes)), vmem((planes, lanes))
    faces = [x_face, x_face, y_face, y_face]
    pair = [vmem((2, rows, lanes))] * 2 + [vmem((2, planes, lanes))] * 2
    dma = pltpu.SemaphoreType.DMA
    work = 40 * planes * rows * lanes

    x0, kappa, *sends = call(
        functools.partial(faces_kernel, sizes), [block, block] + pair, 2, scratch=[dma((2,))], any_in=(0, 1), name="faces"
    )(start_guess, conductivity)
    halos = exchange(sends, sizes)
    r, cx, cy, cz, end = call(
        start_kernel, [block, vmem((planes + 1, rows, lanes)), block, block, block], 3, work,
        scratch=[block, dma((planes // 8,))], any_in=(2,), name="start",
    )(x0, kappa, right_side)
    r, *rest = call(
        functools.partial(start_fix_kernel, sizes), [block] + faces + faces, 9, aliases={0: 0}, name="start_fix"
    )(r, *sends, *halos)
    coeffs, sends = rest[:4], rest[4:]

    vectors, dots = [r], []
    for step in range(M):
        older = [vectors[-2]] if step else []
        last = step == M - 1
        count = 1 + len(older) + 2 * last
        halos = exchange(sends, sizes)
        w, sums = call(
            functools.partial(apply_kernel, len(older), last), [block, vmem((count, 8, 128))], 5 + len(older), work, name="apply"
        )(vectors[-1], cx, cy, cz, end, *older)
        dots.append(sums)
        if last:
            _, payload = call(
                functools.partial(last_fix_kernel, sizes), [block, vmem((devices, 1, 128))], 16, aliases={0: 0}, name="last_fix"
            )(w, *sends, *halos, *coeffs, *dots)
        else:
            w, *sends = call(
                functools.partial(fix_kernel, sizes), [block] + faces, 13, aliases={0: 0}, name="fix"
            )(w, *sends, *halos, *coeffs)
            vectors.append(w)
    sums = lax.all_to_all(payload, ("gx", "gy"), 0, 0, tiled=True)
    out, estimate = call(
        finish_kernel, [jax.ShapeDtypeStruct(shape, F32), jax.ShapeDtypeStruct((1, 128), F32)], 5,
        scratch=[block, dma((planes // 8,))], any_out=(0,), name="finish",
    )(sums, x0, *vectors)
    return out, estimate[0, 0]


def solution(mesh):
    sizes = (mesh.shape["gx"], mesh.shape["gy"])
    in_specs = (P("gx", "gy", None), P("gx", "gy", None), P("gx", "gy", None))
    out_specs = (P("gx", "gy", None), P())
    return jax.shard_map(
        functools.partial(local, sizes), mesh=mesh, in_specs=in_specs, out_specs=out_specs, check_vma=False
    )
```

time: 347 us -> 57.9 us (0.17)
  blocking collectives: 173 us -> 10.6 us
  other arithmetic: 79 us -> 0 us
  waiting for transfers between devices: 26.3 us -> 0.04 us
  Pallas kernels: 0 us -> 26.1 us
  starting transfers between devices: 39.9 us -> 16.9 us
  between operations: 16.7 us -> 0.83 us
  local copies, waits for them, and re-layouts: 10.4 us -> 3.18 us
    psum x4 -> x0, blocking collectives: 173 us -> none  [the longest x3 128 us: local(): lax.psum((local_dots, jnp.sum(vector * vector)), ('gx', 'gy'))]
    reduce_sum x6 -> x0, other arithmetic: 42.7 us -> none  [the longest x2 16.9 us: local(): jnp.sum(vector * basis[earlier])]
    ppermute x20 -> x16, waiting for transfers between devices: 26.3 us -> 0.04 us  [exchange(): lax.ppermute(part, ('gx', 'gy'), pairs)]
    pallas_call x0 -> x10, Pallas kernels: none -> 26.1 us  [the longest x3 16 us: local(): call(functools.partial(apply_kernel, len(older), last), [block, vmem((cou...]
    ppermute x20 -> x16, starting transfers between devices: 39.9 us -> 16.9 us  [exchange(): lax.ppermute(part, ('gx', 'gy'), pairs)]
    concatenate x5 -> x0, other arithmetic: 16.7 us -> none  [with_halo(): jnp.concatenate([lax.ppermute(tail, axis, [(i, (i + 1) % count) for i in...]
    all_to_all x0 -> x1, blocking collectives: none -> 10.6 us  [local(): sums = lax.all_to_all(payload, ('gx', 'gy'), 0, 0, tiled=True)]
    div x3 -> x0, other arithmetic: 10.2 us -> none  [the longest x2 8.35 us: local(): basis.append(vector / length)]
  transfers between devices with their start and end apart: 20 -> 16, of which waited for: 9 -> 0; matrix products, arithmetic and copies ran while one was open for 2% -> 0% of each run, Pallas kernels for 0% -> 38%
where the time goes in v1:
time: 57.9 us; the launch traced here: 57.7 us
  Pallas kernels  26.1 us (45%)
  starting transfers between devices  16.9 us (29%)
  blocking collectives  10.6 us (18%)
  local copies, waits for them, and re-layouts  3.18 us (5%)
  between operations  0.83 us (1%)
    ppermute x16, starting transfers between devices, exchange(): lax.ppermute(part, ('gx', 'gy'), pairs)  16.9 us
    pallas_call x3, Pallas kernels, local(): call(functools.partial(apply_kernel, len(older), last), [block, vmem((cou...  16 us
    all_to_all x1, blocking collectives, local(): sums = lax.all_to_all(payload, ('gx', 'gy'), 0, 0, tiled=True)  10.6 us
    pallas_call x1, Pallas kernels, local(): call(start_kernel, [block, vmem((planes + 1, rows, lanes)), block, block,...  6.08 us
    unnamed x6, local copies, waits for them, and re-layouts  3.18 us
    pallas_call x1, Pallas kernels, local(): call(finish_kernel, [jax.ShapeDtypeStruct(shape, F32), jax.ShapeDtypeStru...  2.24 us
  transfers between devices with their start and end apart: 16, of which 0 were waited for; matrix products, arithmetic and copies ran while one was open for 0% of the time, Pallas kernels for 38%

profile of v1, /device:TPU:0, one launch (start us, length us, event | category | flops | bytes accessed | tf_op | source)
XLA Modules:
  0.0 57.7 jit_solution(3901328710559747110)
XLA Ops:
  0.6 1.6 %copy-done.1 = f32[32,32,512]{2,1,0:T(8,128)S(1)} copy-done((f32[32,32,512]{2,1,0:T(8,128)S(1)}, f32[32,32,512]{2,1,0:T(8,128)}, u32[]{:S(2)}) %copy-start.1) | copy-done | bytes 2097176
  2.2 1.6 %copy-done.2 = f32[32,32,512]{2,1,0:T(8,128)S(1)} copy-done((f32[32,32,512]{2,1,0:T(8,128)S(1)}, f32[32,32,512]{2,1,0:T(8,128)}, u32[]{:S(2)}) %copy-start.2) | copy-done | bytes 2097176
  3.8 0.4 faces.1
  4.2 0.6 collective-permute-start
  4.8 2.6 %collective-permute-start.1 = (f32[2,32,512]{2,1,0:T(8,128)S(1)}, f32[2,32,512]{2,1,0:T(8,128)S(1)}, u32[]{:S(2)}, u32[]{:S(2)}) collective-permute-start(f32[2,32,512]{2,1,0:T(8,128)S(1)} %get-tuple-element.45.sxb), channel_id=1, source_target_pairs={{0,24},{1,25},{2,26},{3,27},{4,28},{5,29},{6,30},{7,31},{8,16},{9,... | collective-permute-start | bytes 393224 | tf_op jit(solution)/shard_map/ppermute | solution.py:52
  7.4 1.5 %collective-permute-start.2 = (f32[2,32,512]{2,1,0:T(8,128)S(1)}, f32[2,32,512]{2,1,0:T(8,128)S(1)}, u32[]{:S(2)}, u32[]{:S(2)}) collective-permute-start(f32[2,32,512]{2,1,0:T(8,128)S(1)} %get-tuple-element.46.sya), channel_id=1, source_target_pairs={{0,1},{1,0},{2,3},{3,2},{4,5},{5,4},{6,7},{7,6},{8,9},{9,8},{10,11... | collective-permute-start | bytes 393224 | tf_op jit(solution)/shard_map/ppermute | solution.py:52
  8.9 6.1 %start.1 = (f32[32,32,512]{2,1,0:T(8,128)S(1)}, f32[33,32,512]{2,1,0:T(8,128)S(1)}, f32[32,32,512]{2,1,0:T(8,128)S(1)}, f32[32,32,512]{2,1,0:T(8,128)S(1)}, f32[32,32,512]{2,1,0:T(8,128)S(1)}) custom-call(f32[32,32,512]{2,1,0:T(8,128)S(1)} %get-tuple-element.41.x_ref, f32[32,32,512]{2,1,0:T(8,128)S(1)} %get-tuple-element.42.k_ref, f32[32,32,512]{2,1,0:T(8,128)S(1)} %copy-done), custom_call_target="tpu_custom_call" | custom-call | flops 20971520 | tf_op jit(solution)/shard_map/start/pallas_call | solution.py:385
  15.0 0.3 start_fix.1
  15.3 0.6 collective-permute-start.4
  15.9 0.2 collective-permute-start.5
  16.0 3.0 %collective-permute-start.6 = (f32[32,512]{1,0:T(8,128)S(1)}, f32[32,512]{1,0:T(8,128)S(1)}, u32[]{:S(2)}, u32[]{:S(2)}) collective-permute-start(f32[32,512]{1,0:T(8,128)S(1)} %get-tuple-element.56.refs_2_), channel_id=1, source_target_pairs={{0,1},{1,0},{2,3},{3,2},{4,5},{5,4},{6,7},{7,6},{8,9},{9,8},{10,11... | collective-permute-start | bytes 196616 | tf_op jit(solution)/shard_map/ppermute | solution.py:52
  19.0 5.2 %apply.3 = (f32[32,32,512]{2,1,0:T(8,128)S(1)}, f32[1,8,128]{2,1,0:T(8,128)S(1)}) custom-call(f32[32,32,512]{2,1,0:T(8,128)S(1)} %get-tuple-element.48.refs_0_.refs_5_.r_ref, f32[33,32,512]{2,1,0:T(8,128)S(1)} %get-tuple-element.49.refs_1_, f32[32,32,512]{2,1,0:T(8,128)S(1)} %get-tuple-element.50.refs_2_, f32[32,32,512]{2,1,0:T(8,128)S(1)} %get-tuple-element.51.refs_3_, ...), custom_call_target="tpu_custom_call" | custom-call | flops 20971520 | tf_op jit(solution)/shard_map/apply/pallas_call | solution.py:400
  24.3 0.2 fix.2
  24.5 0.6 collective-permute-start.8
  25.1 1.2 %collective-permute-start.9 = (f32[32,512]{1,0:T(8,128)S(1)}, f32[32,512]{1,0:T(8,128)S(1)}, u32[]{:S(2)}, u32[]{:S(2)}) collective-permute-start(f32[32,512]{1,0:T(8,128)S(1)} %get-tuple-element.65.refs_1_), channel_id=1, source_target_pairs={{0,24},{1,25},{2,26},{3,27},{4,28},{5,29},{6,30},{7,31},{8,16},{9,... | collective-permute-start | bytes 196616 | tf_op jit(solution)/shard_map/ppermute | solution.py:52
  26.3 3.0 %collective-permute-start.10 = (f32[32,512]{1,0:T(8,128)S(1)}, f32[32,512]{1,0:T(8,128)S(1)}, u32[]{:S(2)}, u32[]{:S(2)}) collective-permute-start(f32[32,512]{1,0:T(8,128)S(1)} %get-tuple-element.66.refs_2_), channel_id=1, source_target_pairs={{0,1},{1,0},{2,3},{3,2},{4,5},{5,4},{6,7},{7,6},{8,9},{9,8},{10,11... | collective-permute-start | bytes 196616 | tf_op jit(solution)/shard_map/ppermute | solution.py:52
  29.2 5.2 %apply.4 = (f32[32,32,512]{2,1,0:T(8,128)S(1)}, f32[2,8,128]{2,1,0:T(8,128)S(1)}) custom-call(f32[32,32,512]{2,1,0:T(8,128)S(1)} %get-tuple-element.62.refs_0_.refs_5_.w1_ref, f32[33,32,512]{2,1,0:T(8,128)S(1)} %get-tuple-element.49.refs_1_, f32[32,32,512]{2,1,0:T(8,128)S(1)} %get-tuple-element.50.refs_2_, f32[32,32,512]{2,1,0:T(8,128)S(1)} %get-tuple-element.51.refs_3_, ...), custom_call_target="tpu_custom_call" | custom-call | flops 20971520 | tf_op jit(solution)/shard_map/apply/pallas_call | solution.py:400
  34.5 0.2 fix.3
  34.8 0.6 collective-permute-start.12
  35.5 3.0 %collective-permute-start.14 = (f32[32,512]{1,0:T(8,128)S(1)}, f32[32,512]{1,0:T(8,128)S(1)}, u32[]{:S(2)}, u32[]{:S(2)}) collective-permute-start(f32[32,512]{1,0:T(8,128)S(1)} %get-tuple-element.72.refs_2_), channel_id=1, source_target_pairs={{0,1},{1,0},{2,3},{3,2},{4,5},{5,4},{6,7},{7,6},{8,9},{9,8},{10,11... | collective-permute-start | bytes 196616 | tf_op jit(solution)/shard_map/ppermute | solution.py:52
  38.5 5.6 %apply.5 = (f32[32,32,512]{2,1,0:T(8,128)S(1)}, f32[4,8,128]{2,1,0:T(8,128)S(1)}) custom-call(f32[32,32,512]{2,1,0:T(8,128)S(1)} %get-tuple-element.68.refs_0_.w2_ref, f32[33,32,512]{2,1,0:T(8,128)S(1)} %get-tuple-element.49.refs_1_, f32[32,32,512]{2,1,0:T(8,128)S(1)} %get-tuple-element.50.refs_2_, f32[32,32,512]{2,1,0:T(8,128)S(1)} %get-tuple-element.51.refs_3_, ...), custom_call_target="tpu_custom_call" | custom-call | flops 20971520 | tf_op jit(solution)/shard_map/apply/pallas_call | solution.py:400
  44.1 0.7 %last_fix.1 = (f32[32,32,512]{2,1,0:T(8,128)S(1)}, f32[32,1,128]{2,1,0:T(1,128)S(1)}) custom-call(f32[32,32,512]{2,1,0:T(8,128)S(1)} %get-tuple-element.69.w_in, f32[32,512]{1,0:T(8,128)S(1)} %get-tuple-element.70.refs_0_, f32[32,512]{1,0:T(8,128)S(1)} %get-tuple-element.71.refs_1_, ...), custom_call_target="tpu_custom_call", output_to_operand_aliasing={{0}: (0, {})} | custom-call | tf_op jit(solution)/shard_map/last_fix/pallas_call | solution.py:405
  44.8 10.6 %all_to_all.5.sums_ref = f32[32,1,128]{2,1,0:T(1,128)S(1)} all-to-all(f32[32,1,128]{2,1,0:T(1,128)S(1)} %get-tuple-element.77), channel_id=1, replica_groups=mesh['gx'=4,'gy'=8] {'gx','gy'}, dimensions={0} | all-to-all | bytes 32768 | tf_op jit(solution)/shard_map/all_to_all | solution.py:413
  55.4 2.2 %finish.1 = (f32[32,32,512]{2,1,0:T(8,128)}, f32[1,128]{1,0:T(1,128)}) custom-call(f32[32,1,128]{2,1,0:T(1,128)S(1)} %all_to_all.5.sums_ref, f32[32,32,512]{2,1,0:T(8,128)S(1)} %get-tuple-element.41.x_ref, f32[32,32,512]{2,1,0:T(8,128)S(1)} %get-tuple-element.48.refs_0_.refs_5_.r_ref, f32[32,32,512]{2,1,0:T(8,128)S(1)} %get-tuple-element.62.refs_0_.refs_5_.w1_ref, ...), custom_call_target="tpu_custom_call" | custom-call | tf_op jit(solution)/shard_map/finish/pallas_call | solution.py:414
  (25 shorter events, 0.2 us)
Async XLA Ops:
  0.6 1.6 %copy-start.1 = (f32[32,32,512]{2,1,0:T(8,128)S(1)}, f32[32,32,512]{2,1,0:T(8,128)}, u32[]{:S(2)}) copy-start(f32[32,32,512]{2,1,0:T(8,128)} %x_hbm.1) | copy-start | bytes 6291460
  2.2 1.6 %copy-start.2 = (f32[32,32,512]{2,1,0:T(8,128)S(1)}, f32[32,32,512]{2,1,0:T(8,128)}, u32[]{:S(2)}) copy-start(f32[32,32,512]{2,1,0:T(8,128)} %k_hbm.1) | copy-start | bytes 6291460
  3.8 5.1 %copy-start = (f32[32,32,512]{2,1,0:T(8,128)S(1)}, f32[32,32,512]{2,1,0:T(8,128)}, u32[]{:S(2)}) copy-start(f32[32,32,512]{2,1,0:T(8,128)} %b_hbm.1) | copy-start | bytes 6291460
  4.2 10.8 %collective-permute-start = (f32[2,32,512]{2,1,0:T(8,128)S(1)}, f32[2,32,512]{2,1,0:T(8,128)S(1)}, u32[]{:S(2)}, u32[]{:S(2)}) collective-permute-start(f32[2,32,512]{2,1,0:T(8,128)S(1)} %get-tuple-element.44.sxa), channel_id=1, source_target_pairs={{0,8},{1,9},{2,10},{3,11},{4,12},{5,13},{6,14},{7,15},{8,0},{9,1},... | collective-permute-start | bytes 393224 | tf_op jit(solution)/shard_map/ppermute | solution.py:52
  4.8 10.2 %collective-permute-start.1 = (f32[2,32,512]{2,1,0:T(8,128)S(1)}, f32[2,32,512]{2,1,0:T(8,128)S(1)}, u32[]{:S(2)}, u32[]{:S(2)}) collective-permute-start(f32[2,32,512]{2,1,0:T(8,128)S(1)} %get-tuple-element.45.sxb), channel_id=1, source_target_pairs={{0,24},{1,25},{2,26},{3,27},{4,28},{5,29},{6,30},{7,31},{8,16},{9,... | collective-permute-start | bytes 393224 | tf_op jit(solution)/shard_map/ppermute | solution.py:52
  7.4 7.6 %collective-permute-start.2 = (f32[2,32,512]{2,1,0:T(8,128)S(1)}, f32[2,32,512]{2,1,0:T(8,128)S(1)}, u32[]{:S(2)}, u32[]{:S(2)}) collective-permute-start(f32[2,32,512]{2,1,0:T(8,128)S(1)} %get-tuple-element.46.sya), channel_id=1, source_target_pairs={{0,1},{1,0},{2,3},{3,2},{4,5},{5,4},{6,7},{7,6},{8,9},{9,8},{10,11... | collective-permute-start | bytes 393224 | tf_op jit(solution)/shard_map/ppermute | solution.py:52
  8.9 6.1 %collective-permute-start.3 = (f32[2,32,512]{2,1,0:T(8,128)S(1)}, f32[2,32,512]{2,1,0:T(8,128)S(1)}, u32[]{:S(2)}, u32[]{:S(2)}) collective-permute-start(f32[2,32,512]{2,1,0:T(8,128)S(1)} %get-tuple-element.47.syb), channel_id=1, source_target_pairs={{0,8},{1,2},{2,1},{3,4},{4,3},{5,6},{6,5},{7,15},{8,0},{9,10},{10,... | collective-permute-start | bytes 393224 | tf_op jit(solution)/shard_map/ppermute | solution.py:52
  15.3 9.0 %collective-permute-start.4 = (f32[32,512]{1,0:T(8,128)S(1)}, f32[32,512]{1,0:T(8,128)S(1)}, u32[]{:S(2)}, u32[]{:S(2)}) collective-permute-start(f32[32,512]{1,0:T(8,128)S(1)} %get-tuple-element.54.refs_0_), channel_id=1, source_target_pairs={{0,8},{1,9},{2,10},{3,11},{4,12},{5,13},{6,14},{7,15},{8,0},{9,1},... | collective-permute-start | bytes 196616 | tf_op jit(solution)/shard_map/ppermute | solution.py:52
  15.9 8.4 %collective-permute-start.5 = (f32[32,512]{1,0:T(8,128)S(1)}, f32[32,512]{1,0:T(8,128)S(1)}, u32[]{:S(2)}, u32[]{:S(2)}) collective-permute-start(f32[32,512]{1,0:T(8,128)S(1)} %get-tuple-element.55.refs_1_), channel_id=1, source_target_pairs={{0,24},{1,25},{2,26},{3,27},{4,28},{5,29},{6,30},{7,31},{8,16},{9,... | collective-permute-start | bytes 196616 | tf_op jit(solution)/shard_map/ppermute | solution.py:52
  16.0 8.2 %collective-permute-start.6 = (f32[32,512]{1,0:T(8,128)S(1)}, f32[32,512]{1,0:T(8,128)S(1)}, u32[]{:S(2)}, u32[]{:S(2)}) collective-permute-start(f32[32,512]{1,0:T(8,128)S(1)} %get-tuple-element.56.refs_2_), channel_id=1, source_target_pairs={{0,1},{1,0},{2,3},{3,2},{4,5},{5,4},{6,7},{7,6},{8,9},{9,8},{10,11... | collective-permute-start | bytes 196616 | tf_op jit(solution)/shard_map/ppermute | solution.py:52
  19.0 5.3 %collective-permute-start.7 = (f32[32,512]{1,0:T(8,128)S(1)}, f32[32,512]{1,0:T(8,128)S(1)}, u32[]{:S(2)}, u32[]{:S(2)}) collective-permute-start(f32[32,512]{1,0:T(8,128)S(1)} %get-tuple-element.57.refs_3_), channel_id=1, source_target_pairs={{0,8},{1,2},{2,1},{3,4},{4,3},{5,6},{6,5},{7,15},{8,0},{9,10},{10,... | collective-permute-start | bytes 196616 | tf_op jit(solution)/shard_map/ppermute | solution.py:52
  24.5 10.0 %collective-permute-start.8 = (f32[32,512]{1,0:T(8,128)S(1)}, f32[32,512]{1,0:T(8,128)S(1)}, u32[]{:S(2)}, u32[]{:S(2)}) collective-permute-start(f32[32,512]{1,0:T(8,128)S(1)} %get-tuple-element.64.refs_0_), channel_id=1, source_target_pairs={{0,8},{1,9},{2,10},{3,11},{4,12},{5,13},{6,14},{7,15},{8,0},{9,1},... | collective-permute-start | bytes 196616 | tf_op jit(solution)/shard_map/ppermute | solution.py:52
  25.1 9.4 %collective-permute-start.9 = (f32[32,512]{1,0:T(8,128)S(1)}, f32[32,512]{1,0:T(8,128)S(1)}, u32[]{:S(2)}, u32[]{:S(2)}) collective-permute-start(f32[32,512]{1,0:T(8,128)S(1)} %get-tuple-element.65.refs_1_), channel_id=1, source_target_pairs={{0,24},{1,25},{2,26},{3,27},{4,28},{5,29},{6,30},{7,31},{8,16},{9,... | collective-permute-start | bytes 196616 | tf_op jit(solution)/shard_map/ppermute | solution.py:52
  26.3 8.2 %collective-permute-start.10 = (f32[32,512]{1,0:T(8,128)S(1)}, f32[32,512]{1,0:T(8,128)S(1)}, u32[]{:S(2)}, u32[]{:S(2)}) collective-permute-start(f32[32,512]{1,0:T(8,128)S(1)} %get-tuple-element.66.refs_2_), channel_id=1, source_target_pairs={{0,1},{1,0},{2,3},{3,2},{4,5},{5,4},{6,7},{7,6},{8,9},{9,8},{10,11... | collective-permute-start | bytes 196616 | tf_op jit(solution)/shard_map/ppermute | solution.py:52
  29.2 5.3 %collective-permute-start.11 = (f32[32,512]{1,0:T(8,128)S(1)}, f32[32,512]{1,0:T(8,128)S(1)}, u32[]{:S(2)}, u32[]{:S(2)}) collective-permute-start(f32[32,512]{1,0:T(8,128)S(1)} %get-tuple-element.67.refs_3_), channel_id=1, source_target_pairs={{0,8},{1,2},{2,1},{3,4},{4,3},{5,6},{6,5},{7,15},{8,0},{9,10},{10,... | collective-permute-start | bytes 196616 | tf_op jit(solution)/shard_map/ppermute | solution.py:52
  34.8 9.3 %collective-permute-start.12 = (f32[32,512]{1,0:T(8,128)S(1)}, f32[32,512]{1,0:T(8,128)S(1)}, u32[]{:S(2)}, u32[]{:S(2)}) collective-permute-start(f32[32,512]{1,0:T(8,128)S(1)} %get-tuple-element.70.refs_0_), channel_id=1, source_target_pairs={{0,8},{1,9},{2,10},{3,11},{4,12},{5,13},{6,14},{7,15},{8,0},{9,1},... | collective-permute-start | bytes 196616 | tf_op jit(solution)/shard_map/ppermute | solution.py:52
  35.3 8.8 %collective-permute-start.13 = (f32[32,512]{1,0:T(8,128)S(1)}, f32[32,512]{1,0:T(8,128)S(1)}, u32[]{:S(2)}, u32[]{:S(2)}) collective-permute-start(f32[32,512]{1,0:T(8,128)S(1)} %get-tuple-element.71.refs_1_), channel_id=1, source_target_pairs={{0,24},{1,25},{2,26},{3,27},{4,28},{5,29},{6,30},{7,31},{8,16},{9,... | collective-permute-start | bytes 196616 | tf_op jit(solution)/shard_map/ppermute | solution.py:52
  35.5 8.6 %collective-permute-start.14 = (f32[32,512]{1,0:T(8,128)S(1)}, f32[32,512]{1,0:T(8,128)S(1)}, u32[]{:S(2)}, u32[]{:S(2)}) collective-permute-start(f32[32,512]{1,0:T(8,128)S(1)} %get-tuple-element.72.refs_2_), channel_id=1, source_target_pairs={{0,1},{1,0},{2,3},{3,2},{4,5},{5,4},{6,7},{7,6},{8,9},{9,8},{10,11... | collective-permute-start | bytes 196616 | tf_op jit(solution)/shard_map/ppermute | solution.py:52
  38.5 5.6 %collective-permute-start.15 = (f32[32,512]{1,0:T(8,128)S(1)}, f32[32,512]{1,0:T(8,128)S(1)}, u32[]{:S(2)}, u32[]{:S(2)}) collective-permute-start(f32[32,512]{1,0:T(8,128)S(1)} %get-tuple-element.73.refs_3_), channel_id=1, source_target_pairs={{0,8},{1,2},{2,1},{3,4},{4,3},{5,6},{6,5},{7,15},{8,0},{9,10},{10,... | collective-permute-start | bytes 196616 | tf_op jit(solution)/shard_map/ppermute | solution.py:52
